TPU v7x, 256 devices: a whole 4x4x8 slice. The times are simulated.
256 devices in a mesh: pix: 256 (over z, y, x, core).
Axes of the slice: x: 4, y: 4, z: 8, core: 2. Of those that a mesh axis runs over, the one named last changes fastest.
Arguments:
- green: float32 [16384, 6144], P('pix'), may hold values from -200 to 200, as said below
- sketch: float32 [6144, 128], P('pix'), may hold values from -0.078125 to 0.078125
Outputs:
- basis: float32 [16384, 128], P('pix')
- projection: float32 [6144, 128], P('pix')
- spectrum_gram: float32 [128, 128], replicated
Inputs may be any that keep to these rules, and one draw needn't show every extreme that they name: `green`: finite real entries; each patch's column has its own scale.
All inputs are finite; a program needn't handle non-finite values.
Results may differ from a plain program's by a relative error of at most 0.000086.
Values sent between devices are 32-bit elements; how exact they have to be, the bound alone decides.
A program may use at most 64 MiB of HBM per device.

v0:
```python
import jax
import jax.numpy as jnp
from jax import lax
from jax.sharding import Mesh
from jax.sharding import PartitionSpec as P

PATCHES = 6144
PIX = ("pix_0", "pix_1", "pix_2", "pix_3")


def in_order(tiles, dim):
    tiles = jnp.moveaxis(tiles, 0, dim)
    dims = tiles.shape
    return tiles.reshape(*dims[:dim], dims[dim] * dims[dim + 1], *dims[dim + 2 :])


def stacked_from(shard, axes, sequence):
    tiles = shard[None]
    for k in sequence:
        tiles = lax.all_gather(tiles, axes[k], axis=0, tiled=True)
    carried = [lax.axis_size(axes[k]) for k in reversed(sequence)]
    tiles = tiles.reshape(*carried, *shard.shape)
    turned = sorted(range(len(sequence)), key=lambda place: sequence[len(sequence) - 1 - place])
    return tiles.transpose(*turned, *range(len(sequence), tiles.ndim)).reshape(-1, *shard.shape)


def whole_of(shard, axes, sequence, dim):
    return in_order(stacked_from(shard, axes, sequence), dim)


def rows_for(lines, size):
    spare = -len(lines) % size
    return jnp.pad(lines, [(0, spare)] + [(0, 0)] * (lines.ndim - 1))


def sent_to_all(shard, axis):
    size = lax.axis_size(axis)
    return lax.all_to_all(
        jnp.broadcast_to(shard[None], (size, *shard.shape)), axis, 0, 0, tiled=True
    )


def whole_of_2(shard, axes, dim):
    far, near = axes
    leading = sent_to_all(shard, far)
    tiles = jnp.swapaxes(sent_to_all(leading, near), 0, 1)
    return in_order(tiles.reshape(-1, *shard.shape), dim)


def in_blocks(shard, dim, size):
    before, after = (shard.shape[:dim], shard.shape[dim + 1 :])
    return jnp.moveaxis(shard.reshape(*before, size, -1, *after), dim, 0)


def summed_on_arrival(shard, axis, dim):
    tiles = in_blocks(shard, dim, lax.axis_size(axis))
    arrived = lax.all_to_all(tiles, axis, split_axis=0, concat_axis=0, tiled=True)
    return arrived.sum(axis=0)


def summed_rows(shard, axes, dim):
    far, near = axes
    own = summed_on_arrival(in_blocks(shard, dim, lax.axis_size(far)), near, dim + 1)
    return jnp.sum(lax.all_to_all(own, far, 0, 0, tiled=True), axis=0)


def total_of(shard, axes):
    lines = shard.reshape(-1)
    padded = rows_for(lines, lax.axis_size(axes[0]) * lax.axis_size(axes[1]))
    whole = whole_of_2(summed_rows(padded, axes, 0), axes, 0)
    return lax.slice_in_dim(whole, 0, len(lines)).reshape(shard.shape)


def body(green, sketch):
    highest = lax.Precision.HIGHEST
    rows_here = green.shape[0]
    devices_pix = lax.axis_size(PIX)
    total_pixels = rows_here * devices_pix
    columns = green
    sketched = jnp.dot(
        columns,
        whole_of(sketch, PIX, (1, 0, 2, 3), 0),
        precision=highest,
        preferred_element_type=jnp.float32,
    )
    local_gram = jnp.dot(
        sketched.T, sketched, precision=highest, preferred_element_type=jnp.float32
    )
    gram = total_of(local_gram, (("pix_0", "pix_1"), ("pix_2", "pix_3")))
    lower = jnp.linalg.cholesky(gram)
    orthonormal = jax.scipy.linalg.solve_triangular(lower, sketched.T, lower=True).T
    columns = green
    projection = summed_rows(
        lax.dot_general(
            columns,
            orthonormal,
            (((0,), (0,)), ((), ())),
            precision=highest,
            preferred_element_type=jnp.float32,
        ),
        (("pix_0", "pix_1"), ("pix_2", "pix_3")),
        0,
    )
    basis = jnp.sqrt(jnp.float32(total_pixels)) * orthonormal
    local_spec = jnp.dot(
        projection.T, projection, precision=highest, preferred_element_type=jnp.float32
    )
    spectrum_gram = total_of(local_spec, (("pix_0", "pix_1"), ("pix_2", "pix_3"))) / jnp.float32(
        PATCHES
    )
    return (basis, projection, spectrum_gram)


def solution(mesh):
    split = Mesh(mesh.devices.reshape(8, 4, 4, 2), ("pix_0", "pix_1", "pix_2", "pix_3"))
    in_specs = (P(PIX, None), P(PIX, None))
    out_specs = (P(PIX, None), P(PIX, None), P())
    return jax.shard_map(body, mesh=split, in_specs=in_specs, out_specs=out_specs, check_vma=False)
```

profile of v0, /device:TPU:1, one launch (start us, length us, event | category | flops | bytes accessed | tf_op | source)
XLA Modules:
  0.0 305.1 jit_solution(14893671459518702312)
XLA Ops:
  7.2 10.7 %all-gather = f32[96,128]{1,0:T(8,128)S(1)} all-gather(f32[24,128]{1,0:T(8,128)} %param.3), channel_id=2, replica_groups=mesh['pix_0'=8,'pix_1'=4,'pix_2'=4,'pix_3'=2] {'pix_1'}, dimensions={0}, use_global_device_ids=true | all-gather | bytes 61440 | tf_op jit(solution)/shard_map/all_gather | solution.py:20
  17.9 24.3 %all_gather.13 = f32[32,24,128]{2,1,0:T(8,128)} all-gather(f32[4,24,128]{2,1,0:T(8,128)S(1)} %bitcast.49), channel_id=1, replica_groups=mesh['pix_0'=8,'pix_1'=4,'pix_2'=4,'pix_3'=2] {'pix_0'}, dimensions={0}, use_global_device_ids=true | all-gather | bytes 442368 | tf_op jit(solution)/shard_map/all_gather | solution.py:20
  42.3 36.8 %all-gather.4.cloned.1.call-done = f32[128,24,128]{2,1,0:T(8,128)} async-done(((f32[32,24,128]{2,1,0:T(8,128)}), f32[128,24,128]{2,1,0:T(8,128)}) %all-gather.4.cloned.1.call-update) | async-done | bytes 1572880 | tf_op jit(solution)/shard_map/all_gather | solution.py:20
  79.1 20.2 %all-gather.6.cloned.1.call-done = f32[256,24,128]{2,1,0:T(8,128)} async-done(((f32[128,24,128]{2,1,0:T(8,128)}), f32[256,24,128]{2,1,0:T(8,128)}) %all-gather.6.cloned.1.call-update) | async-done | bytes 3145744 | tf_op jit(solution)/shard_map/all_gather | solution.py:20
  99.3 2.3 copy.26
  101.6 2.1 fusion.4
  104.2 8.9 %all_to_all.60 = f32[8,1,2048]{2,1,0:T(1,128)S(1)} all-to-all(f32[8,1,2048]{2,1,0:T(1,128)S(1)} %reshape.47), channel_id=1, replica_groups=mesh['pix_0'=8,'pix_1'=4,'pix_2'=4,'pix_3'=2] {'pix_2','pix_3'}, dimensions={0} | all-to-all | bytes 131072 | tf_op jit(solution)/shard_map/all_to_all | solution.py:57
  114.4 18.0 %all_to_all.61 = f32[32,1,64]{2,1,0:T(1,128)S(1)} all-to-all(f32[32,1,64]{2,1,0:T(1,128)S(1)} %bitcast.50), channel_id=1, replica_groups=mesh['pix_0'=8,'pix_1'=4,'pix_2'=4,'pix_3'=2] {'pix_0','pix_1'}, dimensions={0} | all-to-all | bytes 16384 | tf_op jit(solution)/shard_map/all_to_all | solution.py:64
  132.4 11.6 %all_to_all.62 = f32[32,1,64]{2,1,0:T(1,128)S(1)} all-to-all(f32[32,1,64]{2,1,0:T(1,128)S(1)} %broadcast_in_dim.17), channel_id=1, replica_groups=mesh['pix_0'=8,'pix_1'=4,'pix_2'=4,'pix_3'=2] {'pix_0','pix_1'}, dimensions={0} | all-to-all | bytes 16384 | tf_op jit(solution)/shard_map/all_to_all | solution.py:38
  144.2 10.6 %all_to_all.63 = f32[8,1,2048]{2,1,0:T(1,128)S(1)} all-to-all(f32[8,1,2048]{2,1,0:T(1,128)S(1)} %reshape.49), channel_id=1, replica_groups=mesh['pix_0'=8,'pix_1'=4,'pix_2'=4,'pix_3'=2] {'pix_2','pix_3'}, dimensions={0} | all-to-all | bytes 131072 | tf_op jit(solution)/shard_map/all_to_all | solution.py:38
  155.9 11.7 %cholesky.16 = f32[128,128]{1,0:T(8,128)S(1)} custom-call(f32[128,128]{1,0:T(8,128)S(1)} %fusion.3), custom_call_target="Cholesky" | custom-call | tf_op jit(solution)/shard_map/jit(cholesky)/cholesky | solution.py:90
  168.9 9.8 %custom-call.7 = f32[1,128,128]{1,2,0:T(8,128)S(1)} custom-call(f32[1,128,128]{2,1,0:T(8,128)S(1)} %fusion), custom_call_target="InvertDiagBlocksLowerTriangular" | custom-call | tf_op jit(solution)/shard_map/jit(_solve_triangular)/triangular_solve | solution.py:91
  178.9 4.3 %convolution_bitcast_fusion = f32[6144,128]{0,1:T(8,128)} fusion(f32[128,64]{0,1:T(8,128)S(1)} %fusion.1, f32[64,6144]{1,0:T(8,128)S(1)} %copy-done), kind=kOutput, calls=%fused_computation | convolution fusion | flops 603979776 | bytes 4751360 | tf_op jit(solution)/shard_map/dot_general | solution.py:94
  183.2 3.6 %copy.30 = f32[6144,128]{1,0:T(8,128)} copy(f32[6144,128]{0,1:T(8,128)} %convolution_bitcast_fusion) | data formatting | bytes 6291456 | tf_op jit(solution)/shard_map/dot_general | solution.py:94
  186.8 2.1 copy.31
  188.9 41.4 %all_to_all.64 = f32[8,32,24,128]{3,2,1,0:T(8,128)} all-to-all(f32[8,32,24,128]{3,2,1,0:T(8,128)S(1)} %copy.31), channel_id=1, replica_groups=mesh['pix_0'=8,'pix_1'=4,'pix_2'=4,'pix_3'=2] {'pix_2','pix_3'}, dimensions={0} | all-to-all | bytes 6291456 | tf_op jit(solution)/shard_map/all_to_all | solution.py:57
  230.3 2.1 reduce_sum.56
  232.4 16.5 %all_to_all.65 = f32[32,24,128]{2,1,0:T(8,128)S(1)} all-to-all(f32[32,24,128]{2,1,0:T(8,128)S(1)} %reduce_sum.56), channel_id=1, replica_groups=mesh['pix_0'=8,'pix_1'=4,'pix_2'=4,'pix_3'=2] {'pix_0','pix_1'}, dimensions={0} | all-to-all | bytes 786432 | tf_op jit(solution)/shard_map/all_to_all | solution.py:64
  249.5 10.0 %all_to_all.66 = f32[8,1,2048]{2,1,0:T(1,128)S(1)} all-to-all(f32[8,1,2048]{2,1,0:T(1,128)S(1)} %reshape.51), channel_id=1, replica_groups=mesh['pix_0'=8,'pix_1'=4,'pix_2'=4,'pix_3'=2] {'pix_2','pix_3'}, dimensions={0} | all-to-all | bytes 131072 | tf_op jit(solution)/shard_map/all_to_all | solution.py:57
  260.3 12.4 %all_to_all.67 = f32[32,1,64]{2,1,0:T(1,128)S(1)} all-to-all(f32[32,1,64]{2,1,0:T(1,128)S(1)} %bitcast.52), channel_id=1, replica_groups=mesh['pix_0'=8,'pix_1'=4,'pix_2'=4,'pix_3'=2] {'pix_0','pix_1'}, dimensions={0} | all-to-all | bytes 16384 | tf_op jit(solution)/shard_map/all_to_all | solution.py:64
  272.8 11.6 %all_to_all.68 = f32[32,1,64]{2,1,0:T(1,128)S(1)} all-to-all(f32[32,1,64]{2,1,0:T(1,128)S(1)} %broadcast_in_dim.37), channel_id=1, replica_groups=mesh['pix_0'=8,'pix_1'=4,'pix_2'=4,'pix_3'=2] {'pix_0','pix_1'}, dimensions={0} | all-to-all | bytes 16384 | tf_op jit(solution)/shard_map/all_to_all | solution.py:38
  284.4 0.8 reshape.53
  285.1 6.6 %all-to-all-start.9 = ((f32[8,1,2048]{2,1,0:T(1,128)}), f32[8,1,2048]{2,1,0:T(1,128)S(1)}, u32[]{:S(2)}, u32[]{:S(2)}) async-start(f32[8,1,2048]{2,1,0:T(1,128)} %reshape.53), calls=%async_computation.9 | async-start | bytes 131072 | tf_op jit(solution)/shard_map/all_to_all | solution.py:38
  292.3 4.3 %all-to-all-done.9 = f32[8,1,2048]{2,1,0:T(1,128)S(1)} async-done(((f32[8,1,2048]{2,1,0:T(1,128)}), f32[8,1,2048]{2,1,0:T(1,128)S(1)}, u32[]{:S(2)}, u32[]{:S(2)}) %all-to-all-start.9) | async-done | bytes 65568 | tf_op jit(solution)/shard_map/all_to_all | solution.py:38
  (47 shorter events, 8.5 us)
Async XLA Ops:
  7.2 94.4 %copy-start = (f32[64,6144]{1,0:T(8,128)S(1)}, f32[64,6144]{1,0:T(8,128)}, u32[]{:S(2)}) copy-start(f32[64,6144]{1,0:T(8,128)} %param.2) | copy-start | bytes 4718596
  7.2 71.9 %all-gather.4.cloned.1.call-start = ((), (), s32[]{:S(2)}) async-start(), calls=%async_computation.10 | async-start | bytes 1966080 | tf_op jit(solution)/shard_map/all_gather | solution.py:20
  42.3 57.0 %all-gather.6.cloned.1.call-start = ((), (), s32[]{:S(2)}) async-start(), calls=%async_computation.11 | async-start | bytes 4718592 | tf_op jit(solution)/shard_map/all_gather | solution.py:20
  248.9 49.3 %copy-start.1 = (f32[24,128]{1,0:T(8,128)}, f32[24,128]{1,0:T(8,128)S(1)}, u32[]{:S(2)}) copy-start(f32[24,128]{1,0:T(8,128)S(1)} %reduce_sum.57) | copy-start | bytes 36868
  285.1 11.5 %all-to-all-start.9 = ((f32[8,1,2048]{2,1,0:T(1,128)}), f32[8,1,2048]{2,1,0:T(1,128)S(1)}, u32[]{:S(2)}, u32[]{:S(2)}) async-start(f32[8,1,2048]{2,1,0:T(1,128)} %reshape.53), calls=%async_computation.9 | async-start | bytes 131072 | tf_op jit(solution)/shard_map/all_to_all | solution.py:38
Sparse Core Ops, SparseCore 0:
  42.4 36.6 all-gather.3
  80.9 18.3 all-gather.5
where the time goes:
time: 306 us; the launch traced here: 305 us
  blocking collectives  176 us (58%)
  waiting for transfers between devices  61.2 us (20%)
  other arithmetic  28.7 us (9%)
  between operations  14.3 us (5%)
  local copies, waits for them, and re-layouts  11.3 us (4%)
  matrix products  7.14 us (2%)
  starting transfers between devices  6.69 us (2%)
    all_to_all x3, blocking collectives, summed_on_arrival(): lax.all_to_all(tiles, axis, split_axis=0, concat_axis=0, tiled=True)  60.2 us
    all_gather x2, waiting for transfers between devices, stacked_from(): tiles = lax.all_gather(tiles, axes[k], axis=0, tiled=True)  56.9 us
    all_to_all x3, blocking collectives, summed_rows(): return jnp.sum(lax.all_to_all(own, far, 0, 0, tiled=True), axis=0)  46.9 us
    all_gather x2, blocking collectives, stacked_from(): tiles = lax.all_gather(tiles, axes[k], axis=0, tiled=True)  35 us
    all_to_all x3, blocking collectives, sent_to_all(): lax.all_to_all(jnp.broadcast_to(shard[None], (size, *shard.shape)), axis,...  33.8 us
    another operation x3, other arithmetic, body(): lower = jnp.linalg.cholesky(gram)  12.4 us
    another operation x2, other arithmetic, body(): jax.scipy.linalg.solve_triangular(lower, sketched.T, lower=True)  10.5 us
    all_to_all x1, starting transfers between devices, sent_to_all(): lax.all_to_all(jnp.broadcast_to(shard[None], (size, *shard.shape)), axis,...  6.61 us
  transfers between devices with their start and end apart: 3, of which 3 were waited for; matrix products, arithmetic and copies ran while one was open for 0% of the time, Pallas kernels for 0%

commit v1 on v0

--- a/solution.py
+++ b/solution.py
@@ -6,6 +6,11 @@
 
 PATCHES = 6144
 PIX = ("pix_0", "pix_1", "pix_2", "pix_3")
+
+
+def gather_over(x, axis, along):
+    stack = jnp.stack([x] * lax.axis_size(axis))
+    return jnp.concatenate(lax.all_to_all(stack, axis, 0, 0), axis=along)
 
 
 def in_order(tiles, dim):
@@ -17,7 +22,7 @@
 def stacked_from(shard, axes, sequence):
     tiles = shard[None]
     for k in sequence:
-        tiles = lax.all_gather(tiles, axes[k], axis=0, tiled=True)
+        tiles = gather_over(tiles, axes[k], 0)
     carried = [lax.axis_size(axes[k]) for k in reversed(sequence)]
     tiles = tiles.reshape(*carried, *shard.shape)
     turned = sorted(range(len(sequence)), key=lambda place: sequence[len(sequence) - 1 - place])

time: 306 us -> 254 us (0.83)
  waiting for transfers between devices: 61.2 us -> 4.25 us
  blocking collectives: 176 us -> 195 us
  between operations: 14.3 us -> 0.87 us
    all_to_all x0 -> x4, blocking collectives: none -> 60.1 us  [gather_over(): return jnp.concatenate(lax.all_to_all(stack, axis, 0, 0), axis=along)]
    all_gather x2 -> x0, waiting for transfers between devices: 56.9 us -> none  [stacked_from(): tiles = lax.all_gather(tiles, axes[k], axis=0, tiled=True)]
    all_gather x2 -> x0, blocking collectives: 35 us -> none  [stacked_from(): tiles = lax.all_gather(tiles, axes[k], axis=0, tiled=True)]
    all_to_all x3, blocking collectives: 46.9 us -> 42.6 us  [summed_rows(): return jnp.sum(lax.all_to_all(own, far, 0, 0, tiled=True), axis=0)]
  transfers between devices with their start and end apart: 3 -> 1, of which waited for: 3 -> 1; matrix products, arithmetic and copies ran while one was open for 0% -> 0% of each run, Pallas kernels for 0% -> 0%
where the time goes in v1:
time: 254 us
  blocking collectives  195 us (77%)
  other arithmetic  28.9 us (11%)
  local copies, waits for them, and re-layouts  10.3 us (4%)
  matrix products  7.28 us (3%)
  starting transfers between devices  6.61 us (3%)
  waiting for transfers between devices  4.25 us (2%)
    all_to_all x4, blocking collectives, gather_over(): return jnp.concatenate(lax.all_to_all(stack, axis, 0, 0), axis=along)  60.1 us
    all_to_all x3, blocking collectives, summed_on_arrival(): lax.all_to_all(tiles, axis, split_axis=0, concat_axis=0, tiled=True)  58.9 us
    all_to_all x3, blocking collectives, summed_rows(): return jnp.sum(lax.all_to_all(own, far, 0, 0, tiled=True), axis=0)  42.6 us
    all_to_all x3, blocking collectives, sent_to_all(): lax.all_to_all(jnp.broadcast_to(shard[None], (size, *shard.shape)), axis,...  33.8 us
    another operation x3, other arithmetic, body(): lower = jnp.linalg.cholesky(gram)  12.4 us
    another operation x2, other arithmetic, body(): jax.scipy.linalg.solve_triangular(lower, sketched.T, lower=True)  10.5 us
    all_to_all x1, starting transfers between devices, sent_to_all(): lax.all_to_all(jnp.broadcast_to(shard[None], (size, *shard.shape)), axis,...  6.61 us
  transfers between devices with their start and end apart: 1, of which 1 were waited for; matrix products, arithmetic and copies ran while one was open for 0% of the time, Pallas kernels for 0%

profile of v1, /device:TPU:1, one launch (start us, length us, event | category | flops | bytes accessed | tf_op | source)
XLA Modules:
  0.0 253.6 jit_solution(9392008067754099413)
XLA Ops:
  0.6 0.8 stack.12
  1.5 9.2 %all_to_all.80 = f32[4,1,24,128]{3,2,1,0:T(8,128)S(1)} all-to-all(f32[4,1,24,128]{3,2,1,0:T(8,128)S(1)} %stack.12), channel_id=1, replica_groups=mesh['pix_0'=8,'pix_1'=4,'pix_2'=4,'pix_3'=2] {'pix_1'}, dimensions={0} | all-to-all | bytes 98304 | tf_op jit(solution)/shard_map/all_to_all | solution.py:13
  10.7 19.6 %all_to_all.81 = f32[8,4,24,128]{3,2,1,0:T(8,128)S(1)} all-to-all(f32[8,4,24,128]{3,2,1,0:T(8,128)S(1)} %stack.13), channel_id=1, replica_groups=mesh['pix_0'=8,'pix_1'=4,'pix_2'=4,'pix_3'=2] {'pix_0'}, dimensions={0} | all-to-all | bytes 786432 | tf_op jit(solution)/shard_map/all_to_all | solution.py:13
  30.4 20.0 %all_to_all.82 = f32[4,32,24,128]{3,2,1,0:T(8,128)S(1)} all-to-all(f32[4,32,24,128]{3,2,1,0:T(8,128)S(1)} %stack.14), channel_id=1, replica_groups=mesh['pix_0'=8,'pix_1'=4,'pix_2'=4,'pix_3'=2] {'pix_2'}, dimensions={0} | all-to-all | bytes 3145728 | tf_op jit(solution)/shard_map/all_to_all | solution.py:13
  50.6 11.3 %all_to_all.83 = f32[2,128,24,128]{3,2,1,0:T(8,128)S(1)} all-to-all(f32[2,128,24,128]{3,2,1,0:T(8,128)S(1)} %pad_maximum_fusion), channel_id=1, replica_groups=mesh['pix_0'=8,'pix_1'=4,'pix_2'=4,'pix_3'=2] {'pix_3'}, dimensions={0} | all-to-all | bytes 6291456 | tf_op jit(solution)/shard_map/all_to_all | solution.py:13
  62.3 2.2 fusion.4
  65.1 7.6 %all_to_all.84 = f32[8,1,2048]{2,1,0:T(1,128)S(1)} all-to-all(f32[8,1,2048]{2,1,0:T(1,128)S(1)} %reshape.48), channel_id=1, replica_groups=mesh['pix_0'=8,'pix_1'=4,'pix_2'=4,'pix_3'=2] {'pix_2','pix_3'}, dimensions={0} | all-to-all | bytes 131072 | tf_op jit(solution)/shard_map/all_to_all | solution.py:62
  74.0 13.7 %all_to_all.85 = f32[32,1,64]{2,1,0:T(1,128)S(1)} all-to-all(f32[32,1,64]{2,1,0:T(1,128)S(1)} %bitcast.54), channel_id=1, replica_groups=mesh['pix_0'=8,'pix_1'=4,'pix_2'=4,'pix_3'=2] {'pix_0','pix_1'}, dimensions={0} | all-to-all | bytes 16384 | tf_op jit(solution)/shard_map/all_to_all | solution.py:69
  87.8 11.6 %all_to_all.86 = f32[32,1,64]{2,1,0:T(1,128)S(1)} all-to-all(f32[32,1,64]{2,1,0:T(1,128)S(1)} %broadcast_in_dim.14), channel_id=1, replica_groups=mesh['pix_0'=8,'pix_1'=4,'pix_2'=4,'pix_3'=2] {'pix_0','pix_1'}, dimensions={0} | all-to-all | bytes 16384 | tf_op jit(solution)/shard_map/all_to_all | solution.py:43
  99.5 10.6 %all_to_all.87 = f32[8,1,2048]{2,1,0:T(1,128)S(1)} all-to-all(f32[8,1,2048]{2,1,0:T(1,128)S(1)} %reshape.50), channel_id=1, replica_groups=mesh['pix_0'=8,'pix_1'=4,'pix_2'=4,'pix_3'=2] {'pix_2','pix_3'}, dimensions={0} | all-to-all | bytes 131072 | tf_op jit(solution)/shard_map/all_to_all | solution.py:43
  111.2 11.7 %cholesky.16 = f32[128,128]{1,0:T(8,128)S(1)} custom-call(f32[128,128]{1,0:T(8,128)S(1)} %fusion.3), custom_call_target="Cholesky" | custom-call | tf_op jit(solution)/shard_map/jit(cholesky)/cholesky | solution.py:95
  124.3 9.8 %custom-call.7 = f32[1,128,128]{1,2,0:T(8,128)S(1)} custom-call(f32[1,128,128]{2,1,0:T(8,128)S(1)} %fusion), custom_call_target="InvertDiagBlocksLowerTriangular" | custom-call | tf_op jit(solution)/shard_map/jit(_solve_triangular)/triangular_solve | solution.py:96
  134.3 4.3 %convolution_bitcast_fusion = f32[6144,128]{0,1:T(8,128)} fusion(f32[128,64]{0,1:T(8,128)S(1)} %fusion.1, f32[64,6144]{1,0:T(8,128)S(1)} %copy-done), kind=kOutput, calls=%fused_computation | convolution fusion | flops 603979776 | bytes 4751360 | tf_op jit(solution)/shard_map/dot_general | solution.py:99
  138.6 3.6 %copy.30 = f32[6144,128]{1,0:T(8,128)} copy(f32[6144,128]{0,1:T(8,128)} %convolution_bitcast_fusion) | data formatting | bytes 6291456 | tf_op jit(solution)/shard_map/dot_general | solution.py:99
  142.2 2.1 copy.31
  144.3 41.4 %all_to_all.88 = f32[8,32,24,128]{3,2,1,0:T(8,128)} all-to-all(f32[8,32,24,128]{3,2,1,0:T(8,128)S(1)} %copy.31), channel_id=1, replica_groups=mesh['pix_0'=8,'pix_1'=4,'pix_2'=4,'pix_3'=2] {'pix_2','pix_3'}, dimensions={0} | all-to-all | bytes 6291456 | tf_op jit(solution)/shard_map/all_to_all | solution.py:62
  185.7 2.1 reduce_sum.56
  187.8 16.5 %all_to_all.89 = f32[32,24,128]{2,1,0:T(8,128)S(1)} all-to-all(f32[32,24,128]{2,1,0:T(8,128)S(1)} %reduce_sum.56), channel_id=1, replica_groups=mesh['pix_0'=8,'pix_1'=4,'pix_2'=4,'pix_3'=2] {'pix_0','pix_1'}, dimensions={0} | all-to-all | bytes 786432 | tf_op jit(solution)/shard_map/all_to_all | solution.py:69
  204.8 10.0 %all_to_all.90 = f32[8,1,2048]{2,1,0:T(1,128)S(1)} all-to-all(f32[8,1,2048]{2,1,0:T(1,128)S(1)} %reshape.52), channel_id=1, replica_groups=mesh['pix_0'=8,'pix_1'=4,'pix_2'=4,'pix_3'=2] {'pix_2','pix_3'}, dimensions={0} | all-to-all | bytes 131072 | tf_op jit(solution)/shard_map/all_to_all | solution.py:62
  215.6 12.4 %all_to_all.91 = f32[32,1,64]{2,1,0:T(1,128)S(1)} all-to-all(f32[32,1,64]{2,1,0:T(1,128)S(1)} %bitcast.56), channel_id=1, replica_groups=mesh['pix_0'=8,'pix_1'=4,'pix_2'=4,'pix_3'=2] {'pix_0','pix_1'}, dimensions={0} | all-to-all | bytes 16384 | tf_op jit(solution)/shard_map/all_to_all | solution.py:69
  228.1 11.6 %all_to_all.92 = f32[32,1,64]{2,1,0:T(1,128)S(1)} all-to-all(f32[32,1,64]{2,1,0:T(1,128)S(1)} %broadcast_in_dim.17), channel_id=1, replica_groups=mesh['pix_0'=8,'pix_1'=4,'pix_2'=4,'pix_3'=2] {'pix_0','pix_1'}, dimensions={0} | all-to-all | bytes 16384 | tf_op jit(solution)/shard_map/all_to_all | solution.py:43
  239.7 0.8 reshape.54
  240.5 6.6 %all-to-all-start.13 = ((f32[8,1,2048]{2,1,0:T(1,128)}), f32[8,1,2048]{2,1,0:T(1,128)S(1)}, u32[]{:S(2)}, u32[]{:S(2)}) async-start(f32[8,1,2048]{2,1,0:T(1,128)} %reshape.54), calls=%async_computation.13 | async-start | bytes 131072 | tf_op jit(solution)/shard_map/all_to_all | solution.py:43
  247.7 4.3 %all-to-all-done.13 = f32[8,1,2048]{2,1,0:T(1,128)S(1)} async-done(((f32[8,1,2048]{2,1,0:T(1,128)}), f32[8,1,2048]{2,1,0:T(1,128)S(1)}, u32[]{:S(2)}, u32[]{:S(2)}) %all-to-all-start.13) | async-done | bytes 65568 | tf_op jit(solution)/shard_map/all_to_all | solution.py:43
  (47 shorter events, 9.1 us)
Async XLA Ops:
  0.6 61.7 %copy-start = (f32[64,6144]{1,0:T(8,128)S(1)}, f32[64,6144]{1,0:T(8,128)}, u32[]{:S(2)}) copy-start(f32[64,6144]{1,0:T(8,128)} %param.2) | copy-start | bytes 4718596
  204.3 49.3 %copy-start.1 = (f32[24,128]{1,0:T(8,128)}, f32[24,128]{1,0:T(8,128)S(1)}, u32[]{:S(2)}) copy-start(f32[24,128]{1,0:T(8,128)S(1)} %reduce_sum.57) | copy-start | bytes 36868
  240.5 11.5 %all-to-all-start.13 = ((f32[8,1,2048]{2,1,0:T(1,128)}), f32[8,1,2048]{2,1,0:T(1,128)S(1)}, u32[]{:S(2)}, u32[]{:S(2)}) async-start(f32[8,1,2048]{2,1,0:T(1,128)} %reshape.54), calls=%async_computation.13 | async-start | bytes 131072 | tf_op jit(solution)/shard_map/all_to_all | solution.py:43
